TPU v7x, 32 devices: a whole 2x2x4 slice. The times are simulated.
32 devices in a mesh: row: 2 (over x), col: 4 (over y, core), depth: 4 (over z).
Axes of the slice: x: 2, y: 2, z: 4, core: 2. Of those that a mesh axis runs over, the one named last changes fastest.
Arguments:
- left_values: bfloat16 [96, 32, 4, 529], P('row', ('col', 'depth')), may hold values from -1.25 to 1.25
- left_columns: int32 [96, 32, 4], P('row', ('col', 'depth')), may hold values from 0 to 39, as said below
- right_values: bfloat16 [32, 40, 4, 3, 529], P(('col', 'depth'), 'row'), may hold values from -1.75 to 1.75
- right_columns: int32 [32, 40, 4, 3], P(('col', 'depth'), 'row'), may hold values from 0 to 31, as said below
Outputs:
- product_matrix: bfloat16 [2208, 2944], P('row', ('col', 'depth'))
Inputs may be any that keep to these rules, and one draw needn't show every extreme that they name: `left_columns`: within one block row and panel the 4 entries are distinct. `right_columns`: within one block row and column tile the 3 entries are distinct.
All inputs are finite; a program needn't handle non-finite values.
Results may differ from a plain program's by a relative error of at most 0.001.
Values may be sent and summed in bfloat16 or wider, within the bound.
A program may use at most 192 MiB of HBM per device.

v0:
```python
import math
import jax
import jax.numpy as jnp
from jax import lax
from jax.sharding import PartitionSpec as P

PANEL = 40
CTW = 32


def dense_left(values, columns, panel_width):
    rows_here, panels, slots, square = values.shape
    block_edge = math.isqrt(square)
    onehot = (
        columns.astype(jnp.float32)[..., None] == jnp.arange(panel_width, dtype=jnp.float32)
    ).astype(jnp.bfloat16)
    blocks = values.reshape(rows_here, panels, slots, block_edge, block_edge)
    filled = jnp.einsum(
        "mqsp,mqsab->qmapb", onehot, blocks, preferred_element_type=jnp.float32
    ).astype(jnp.bfloat16)
    return filled.reshape(panels, rows_here * block_edge, panel_width * block_edge)


def dense_right(values, columns, tile_width):
    panels, rows_here, tiles, slots, square = values.shape
    block_edge = math.isqrt(square)
    onehot = (
        columns.astype(jnp.float32)[..., None] == jnp.arange(tile_width, dtype=jnp.float32)
    ).astype(jnp.bfloat16)
    blocks = values.reshape(panels, rows_here, tiles, slots, block_edge, block_edge)
    filled = jnp.einsum(
        "qrtuc,qrtuab->qratcb", onehot, blocks, preferred_element_type=jnp.float32
    ).astype(jnp.bfloat16)
    return filled.reshape(panels, rows_here * block_edge, tiles * tile_width * block_edge)


def contract(left_values, left_codes, right_values, right_codes):
    left_filled = dense_left(left_values, left_codes, PANEL)
    right_filled = dense_right(
        lax.all_gather(right_values, "row", axis=1, tiled=True),
        lax.all_gather(right_codes, "row", axis=1, tiled=True),
        CTW,
    )
    return jnp.einsum("qmk,qkn->mn", left_filled, right_filled, preferred_element_type=jnp.float32)


def body(left_values, left_columns, right_values, right_columns):
    right_codes = right_columns.astype(jnp.bfloat16)
    partial_sums = contract(left_values, left_columns, right_values, right_codes)
    result = lax.psum_scatter(partial_sums, ("col", "depth"), scatter_dimension=1, tiled=True)
    return result.astype(jnp.bfloat16)


def solution(mesh):
    placed = (
        P("row", ("col", "depth"), None, None),
        P("row", ("col", "depth"), None),
        P(("col", "depth"), "row", None, None, None),
        P(("col", "depth"), "row", None, None),
    )
    return jax.shard_map(
        body, mesh=mesh, in_specs=placed, out_specs=P("row", ("col", "depth")), check_vma=False
    )
```

profile of v0, /device:TPU:0, one launch (start us, length us, event | category | flops | bytes accessed | tf_op | source)
XLA Modules:
  0.0 491.5 jit_solution(12231086556347016809)
XLA Ops:
  6.5 0.0 reduce-scatter.4.cloned.1.call-start
  6.5 21.0 %all_gather.7 = bf16[2,40,4,3,529]{4,2,3,1,0:T(4,128)(2,1)} all-gather(bf16[2,20,4,3,529]{4,2,3,1,0:T(4,128)(2,1)} %param.6), channel_id=1, replica_groups=mesh['row'=2,'col'=4,'depth'=4] {'row'}, dimensions={1}, use_global_device_ids=true | all-gather | bytes 1523520 | tf_op jit(solution)/shard_map/all_gather | solution.py:40
  27.5 0.0 copy-start.1
  27.5 4.9 %copy.32 = bf16[2,40,4,3,529]{1,2,4,3,0:T(4,128)(2,1)S(1)} copy(bf16[2,40,4,3,529]{4,2,3,1,0:T(4,128)(2,1)} %all_gather.7) | data formatting | bytes 2031360 | tf_op jit(solution)/shard_map/all_gather | solution.py:40
  32.4 11.9 %copy.33 = bf16[2,40,4,3,23,23]{5,3,4,2,1,0:T(4,128)(2,1)} copy(bf16[2,40,4,3,23,23]{1,2,5,4,3,0:T(4,128)(2,1)S(1)} %bitcast.33) | data formatting | bytes 2031360 | tf_op jit(solution)/shard_map/reshape | solution.py:30
  44.3 0.0 copy-done.1
  44.3 0.1 copy.29
  44.4 4.5 all_gather.6
  49.0 0.1 copy.30
  49.1 0.2 copy.31
  49.3 31.1 %convert_bitcast_fusion = bf16[2,40,23,4,32,23]{4,5,2,3,1,0:T(8,128)(2,1)} fusion(bf16[2,40,4,3,23,23]{5,3,4,2,1,0:T(4,128)(2,1)} %copy.33, f32[2,40,4,3]{3,2,1,0:T(4,128)S(1)} %copy.31), kind=kOutput, calls=%fused_computation | convolution fusion | flops 37949440 | bytes 11853440 | tf_op jit(solution)/shard_map/qrtuc,qrtuab->qratcb/dot_general | solution.py:31
  80.4 80.8 %copy.34 = bf16[2,40,23,4,32,23]{5,4,3,2,1,0:T(8,128)(2,1)} copy(bf16[2,40,23,4,32,23]{4,5,2,3,1,0:T(8,128)(2,1)} %convert_bitcast_fusion) | data formatting | bytes 21667840 | tf_op jit(solution)/shard_map/convert_element_type | solution.py:33
  161.2 0.0 copy-start
  161.2 0.0 copy-start.2
  161.2 70.7 %reshape.17 = bf16[2,920,2944]{2,1,0:T(8,128)(2,1)} reshape(bf16[2,40,23,4,32,23]{5,4,3,2,1,0:T(8,128)(2,1)} %copy.34) | data formatting | bytes 21667840 | tf_op jit(solution)/shard_map/reshape | solution.py:34
  231.9 0.0 copy-done
  231.9 1.7 copy.26
  233.6 3.6 copy.27
  237.2 0.0 copy-done.2
  237.2 0.1 copy.25
  237.3 10.2 %fusion = bf16[2,48,23,40,23]{3,4,2,1,0:T(8,128)(2,1)} fusion(bf16[48,2,4,23,23]{4,2,3,0,1:T(4,128)(2,1)S(1)} %copy.27, f32[48,2,4]{2,0,1:T(8,128)S(1)} %copy.25), kind=kOutput, calls=%fused_computation.3 | convolution fusion | flops 18297600 | bytes 4470528 | tf_op jit(solution)/shard_map/mqsp,mqsab->qmapb/dot_general | solution.py:18
  247.5 45.4 %copy.28 = bf16[2,48,23,40,23]{2,1,4,3,0:T(8,128)(2,1)} copy(bf16[2,48,23,40,23]{3,4,2,1,0:T(8,128)(2,1)} %fusion) | data formatting | bytes 8125440 | tf_op jit(solution)/shard_map/convert_element_type | solution.py:20
  292.9 27.5 %reshape.15 = bf16[2,1104,920]{1,2,0:T(8,128)(2,1)} reshape(bf16[2,48,23,40,23]{2,1,4,3,0:T(8,128)(2,1)} %copy.28) | data formatting | bytes 8125440 | tf_op jit(solution)/shard_map/reshape | solution.py:21
  320.3 21.8 %convolution_bitcast_fusion = f32[1104,2944]{0,1:T(8,128)} fusion(bf16[2,1104,920]{1,2,0:T(8,128)(2,1)} %reshape.15, bf16[2,920,2944]{2,1,0:T(8,128)(2,1)} %reshape.17), kind=kOutput, calls=%fused_computation.2 | convolution fusion | flops 11960647680 | bytes 27897344 | tf_op jit(solution)/shard_map/qmk,qkn->mn/dot_general | solution.py:44
  342.1 0.0 reduce-scatter.4.cloned.1.call-update
  342.1 140.6 %reduce-scatter.4.cloned.1.call-done = f32[1104,184]{0,1:T(8,128)} async-done(((f32[1104,2944]{0,1:T(8,128)}), f32[1104,184]{0,1:T(8,128)}) %reduce-scatter.4.cloned.1.call-update) | async-done | bytes 812560
  482.7 2.0 convert_element_type.33
  (2 shorter events, 0.0 us)
Async XLA Ops:
  6.5 476.1 %reduce-scatter.4.cloned.1.call-start = ((), (), s32[]{:S(2)}) async-start(), calls=%async_computation.1 | async-start | bytes 14413824
  27.5 16.8 %copy-start.1 = (s32[2,20,4,3]{1,2,3,0:T(4,128)S(1)}, s32[2,20,4,3]{1,2,3,0:T(4,128)}, u32[]{:S(2)}) copy-start(s32[2,20,4,3]{1,2,3,0:T(4,128)} %param.7) | copy-start | bytes 5764
  161.2 70.7 %copy-start = (bf16[48,2,4,529]{3,2,1,0:T(4,128)(2,1)S(1)}, bf16[48,2,4,529]{3,2,1,0:T(4,128)(2,1)}, u32[]{:S(2)}) copy-start(bf16[48,2,4,529]{3,2,1,0:T(4,128)(2,1)} %param.4) | copy-start | bytes 1218820
  161.2 75.9 %copy-start.2 = (s32[48,2,4]{0,2,1:T(4,128)S(1)}, s32[48,2,4]{0,2,1:T(4,128)}, u32[]{:S(2)}) copy-start(s32[48,2,4]{0,2,1:T(4,128)} %param.5) | copy-start | bytes 4612
Sparse Core Ops, SparseCore 0:
  342.2 140.3 reduce-scatter.3
where the time goes:
time: 497 us; the launch traced here: 491 us
  local copies, waits for them, and re-layouts  247 us (50%)
  waiting for transfers between devices  141 us (28%)
  matrix products  63.1 us (13%)
  blocking collectives  25.5 us (5%)
  between operations  13.4 us (3%)
    unnamed x2, waiting for transfers between devices  141 us
    convert_element_type x1, local copies, waits for them, and re-layouts, dense_right(): filled = jnp.einsum('qrtuc,qrtuab->qratcb', onehot, blocks, preferred_ele...  80.8 us
    reshape x1, local copies, waits for them, and re-layouts, dense_right(): filled.reshape(panels, rows_here * block_edge, tiles * tile_width * block...  70.7 us
    convert_element_type x1, local copies, waits for them, and re-layouts, dense_left(): filled = jnp.einsum('mqsp,mqsab->qmapb', onehot, blocks, preferred_elemen...  45.4 us
    dot_general x1, matrix products, dense_right(): jnp.einsum('qrtuc,qrtuab->qratcb', onehot, blocks, preferred_element_type...  31.1 us
    reshape x1, local copies, waits for them, and re-layouts, dense_left(): filled.reshape(panels, rows_here * block_edge, panel_width * block_edge)  27.5 us
    dot_general x1, matrix products, contract(): jnp.einsum('qmk,qkn->mn', left_filled, right_filled, preferred_element_ty...  21.8 us
    all_gather x1, blocking collectives, contract(): lax.all_gather(right_values, 'row', axis=1, tiled=True)  21 us
  transfers between devices with their start and end apart: 1, of which 1 were waited for; matrix products, arithmetic and copies ran while one was open for 0% of the time, Pallas kernels for 0%

commit v1 on v0

--- a/solution.py
+++ b/solution.py
@@ -37,7 +37,7 @@
 def contract(left_values, left_codes, right_values, right_codes):
     left_filled = dense_left(left_values, left_codes, PANEL)
     right_filled = dense_right(
-        lax.all_gather(right_values, "row", axis=1, tiled=True),
+        jnp.concatenate(lax.all_gather(right_values, "row"), axis=1),
         lax.all_gather(right_codes, "row", axis=1, tiled=True),
         CTW,
     )

time: 497 us -> 486 us (0.978)
  local copies, waits for them, and re-layouts: 247 us -> 237 us
    reshape x1 -> x0, local copies, waits for them, and re-layouts: 11.9 us -> none  [dense_right(): values.reshape(panels, rows_here, tiles, slots, block_edge, block_edge)]
    another operation x0 -> x1, local copies, waits for them, and re-layouts: none -> 6.59 us  [dense_right(): values.reshape(panels, rows_here, tiles, slots, block_edge, block_edge)]
where the time goes in v1:
time: 486 us; the launch traced here: 480 us
  local copies, waits for them, and re-layouts  237 us (49%)
  waiting for transfers between devices  142 us (29%)
  matrix products  62.7 us (13%)
  blocking collectives  22.4 us (5%)
  between operations  13.4 us (3%)
    unnamed x2, waiting for transfers between devices  142 us
    convert_element_type x1, local copies, waits for them, and re-layouts, dense_right(): filled = jnp.einsum('qrtuc,qrtuab->qratcb', onehot, blocks, preferred_ele...  80.8 us
    reshape x1, local copies, waits for them, and re-layouts, dense_right(): filled.reshape(panels, rows_here * block_edge, tiles * tile_width * block...  70.7 us
    convert_element_type x1, local copies, waits for them, and re-layouts, dense_left(): filled = jnp.einsum('mqsp,mqsab->qmapb', onehot, blocks, preferred_elemen...  45.4 us
    dot_general x1, matrix products, dense_right(): jnp.einsum('qrtuc,qrtuab->qratcb', onehot, blocks, preferred_element_type...  30.8 us
    reshape x1, local copies, waits for them, and re-layouts, dense_left(): filled.reshape(panels, rows_here * block_edge, panel_width * block_edge)  27.5 us
    dot_general x1, matrix products, contract(): jnp.einsum('qmk,qkn->mn', left_filled, right_filled, preferred_element_ty...  21.7 us
    all_gather x1, blocking collectives, contract(): lax.all_gather(right_values, 'row')  17.9 us
  transfers between devices with their start and end apart: 1, of which 1 were waited for; matrix products, arithmetic and copies ran while one was open for 0% of the time, Pallas kernels for 0%

profile of v1, /device:TPU:0, one launch (start us, length us, event | category | flops | bytes accessed | tf_op | source)
XLA Modules:
  0.0 480.0 jit_solution(10411567976000572632)
XLA Ops:
  6.5 0.0 copy-start.1
  6.5 0.0 reduce-scatter.4.cloned.1.call-start
  6.5 17.9 %all-gather = bf16[4,20,4,3,529]{4,2,3,1,0:T(4,128)(2,1)S(1)} all-gather(bf16[2,20,4,3,529]{4,2,3,1,0:T(4,128)(2,1)} %param.6), channel_id=2, replica_groups=mesh['row'=2,'col'=4,'depth'=4] {'row'}, dimensions={0}, use_global_device_ids=true | all-gather | bytes 1523520 | tf_op jit(solution)/shard_map/all_gather | solution.py:40
  24.4 0.4 copy.41
  24.8 6.6 %reshape_reshape.3 = bf16[2,40,4,3,23,23]{5,4,2,3,1,0:T(8,128)(2,1)} reshape(bf16[2,2,20,4,3,529]{5,3,4,2,1,0:T(4,128)(2,1)S(1)} %bitcast.36) | data formatting | bytes 2031360 | tf_op jit(solution)/shard_map/reshape;reshape | solution.py:30
  31.4 0.0 copy-done.1
  31.4 0.1 copy.29
  31.6 4.5 all_gather.9
  36.1 0.1 copy.30
  36.3 0.2 copy.31
  36.4 30.8 %convert_bitcast_fusion = bf16[2,40,23,4,32,23]{4,5,2,3,1,0:T(8,128)(2,1)} fusion(bf16[2,40,4,3,23,23]{5,4,2,3,1,0:T(8,128)(2,1)} %reshape_reshape.3, f32[2,40,4,3]{3,2,1,0:T(4,128)S(1)} %copy.31), kind=kOutput, calls=%fused_computation | convolution fusion | flops 37949440 | bytes 11853440 | tf_op jit(solution)/shard_map/qrtuc,qrtuab->qratcb/dot_general | solution.py:31
  67.2 80.8 %copy.34 = bf16[2,40,23,4,32,23]{5,4,3,2,1,0:T(8,128)(2,1)} copy(bf16[2,40,23,4,32,23]{4,5,2,3,1,0:T(8,128)(2,1)} %convert_bitcast_fusion) | data formatting | bytes 21667840 | tf_op jit(solution)/shard_map/convert_element_type | solution.py:33
  148.0 0.0 copy-start
  148.0 0.0 copy-start.2
  148.0 70.7 %reshape.17 = bf16[2,920,2944]{2,1,0:T(8,128)(2,1)} reshape(bf16[2,40,23,4,32,23]{5,4,3,2,1,0:T(8,128)(2,1)} %copy.34) | data formatting | bytes 21667840 | tf_op jit(solution)/shard_map/reshape | solution.py:34
  218.7 0.0 copy-done
  218.7 1.7 copy.26
  220.4 3.6 copy.27
  223.9 0.0 copy-done.2
  223.9 0.1 copy.25
  224.0 10.2 %fusion = bf16[2,48,23,40,23]{3,4,2,1,0:T(8,128)(2,1)} fusion(bf16[48,2,4,23,23]{4,2,3,0,1:T(4,128)(2,1)S(1)} %copy.27, f32[48,2,4]{2,0,1:T(8,128)S(1)} %copy.25), kind=kOutput, calls=%fused_computation.3 | convolution fusion | flops 18297600 | bytes 4470528 | tf_op jit(solution)/shard_map/mqsp,mqsab->qmapb/dot_general | solution.py:18
  234.2 45.4 %copy.28 = bf16[2,48,23,40,23]{2,1,4,3,0:T(8,128)(2,1)} copy(bf16[2,48,23,40,23]{3,4,2,1,0:T(8,128)(2,1)} %fusion) | data formatting | bytes 8125440 | tf_op jit(solution)/shard_map/convert_element_type | solution.py:20
  279.6 27.5 %reshape.15 = bf16[2,1104,920]{1,2,0:T(8,128)(2,1)} reshape(bf16[2,48,23,40,23]{2,1,4,3,0:T(8,128)(2,1)} %copy.28) | data formatting | bytes 8125440 | tf_op jit(solution)/shard_map/reshape | solution.py:21
  307.1 21.7 %convolution_bitcast_fusion = f32[1104,2944]{0,1:T(8,128)} fusion(bf16[2,1104,920]{1,2,0:T(8,128)(2,1)} %reshape.15, bf16[2,920,2944]{2,1,0:T(8,128)(2,1)} %reshape.17), kind=kOutput, calls=%fused_computation.2 | convolution fusion | flops 11960647680 | bytes 27897344 | tf_op jit(solution)/shard_map/qmk,qkn->mn/dot_general | solution.py:44
  328.8 0.0 reduce-scatter.4.cloned.1.call-update
  328.9 142.4 %reduce-scatter.4.cloned.1.call-done = f32[1104,184]{0,1:T(8,128)} async-done(((f32[1104,2944]{0,1:T(8,128)}), f32[1104,184]{0,1:T(8,128)}) %reduce-scatter.4.cloned.1.call-update) | async-done | bytes 812560
  471.2 2.0 convert_element_type.33
  (2 shorter events, 0.0 us)
Async XLA Ops:
  6.5 24.9 %copy-start.1 = (s32[2,20,4,3]{1,2,3,0:T(4,128)S(1)}, s32[2,20,4,3]{1,2,3,0:T(4,128)}, u32[]{:S(2)}) copy-start(s32[2,20,4,3]{1,2,3,0:T(4,128)} %param.7) | copy-start | bytes 5764
  6.5 464.7 %reduce-scatter.4.cloned.1.call-start = ((), (), s32[]{:S(2)}) async-start(), calls=%async_computation.1 | async-start | bytes 14413824
  148.0 70.7 %copy-start = (bf16[48,2,4,529]{3,2,1,0:T(4,128)(2,1)S(1)}, bf16[48,2,4,529]{3,2,1,0:T(4,128)(2,1)}, u32[]{:S(2)}) copy-start(bf16[48,2,4,529]{3,2,1,0:T(4,128)(2,1)} %param.4) | copy-start | bytes 1218820
  148.0 75.9 %copy-start.2 = (s32[48,2,4]{0,2,1:T(4,128)S(1)}, s32[48,2,4]{0,2,1:T(4,128)}, u32[]{:S(2)}) copy-start(s32[48,2,4]{0,2,1:T(4,128)} %param.5) | copy-start | bytes 4612
Sparse Core Ops, SparseCore 0:
  329.0 142.1 reduce-scatter.3
